TPU v7x, 8 devices: a whole 2x2x1 slice. The times are simulated.
8 devices in a mesh: fsdp: 8 (over z, y, x, core).
Axes of the slice: x: 2, y: 2, z: 1, core: 2. Of those that a mesh axis runs over, the one named last changes fastest.
Arguments:
- tokens: int32 [8, 512], P('fsdp')
- embed_table: float32 [49152, 2048], P('fsdp')
- norm_gain: float32 [2048], P('fsdp')
- w_query: float32 [2048, 2048], P('fsdp')
- w_key: float32 [2048, 2048], P('fsdp')
- w_value: float32 [2048, 2048], P('fsdp')
- d_query: bfloat16 [8, 512, 2048], P('fsdp')
- d_key: bfloat16 [8, 512, 2048], P('fsdp')
- d_value: bfloat16 [8, 512, 2048], P('fsdp')
Outputs:
- output 1: bfloat16 [8, 512, 2048], P('fsdp')
- output 2: bfloat16 [8, 512, 2048], P('fsdp')
- output 3: bfloat16 [8, 512, 2048], P('fsdp')
- output 4: float32 [49152, 2048], P('fsdp')
- output 5: float32 [2048], P('fsdp')
- output 6: float32 [2048, 2048], P('fsdp')
- output 7: float32 [2048, 2048], P('fsdp')
- output 8: float32 [2048, 2048], P('fsdp')
All inputs are finite; a program needn't handle non-finite values.
Results may differ from a plain program's by a relative error of at most 0.00413466.
Values are sent between devices in bfloat16 or wider.
A program may use at most 1 GiB of HBM per device.

v0:
```python
import jax
import jax.numpy as jnp
from jax import lax
from jax.sharding import PartitionSpec as P

AXIS_NAME = "fsdp"


def norm_forward(x_rows, gain_full):
    inv_rms = lax.rsqrt(jnp.mean(x_rows * x_rows, axis=-1, keepdims=True) + 1e-5)
    h_rows = x_rows * inv_rms
    return inv_rms, h_rows, (h_rows * gain_full).astype(jnp.bfloat16)


def solution(mesh):
    def local_step(tokens, embed_shard, gain_shard, wq_shard, wk_shard, wv_shard, d_query, d_key, d_value):
        vocab_local = embed_shard.shape[0]
        dev_index = lax.axis_index(AXIS_NAME)
        all_tokens = lax.all_gather(tokens, AXIS_NAME, axis=0, tiled=True)
        local_ids = all_tokens - dev_index * vocab_local
        is_owned = (local_ids >= 0) & (local_ids < vocab_local)
        owned_rows = jnp.take(embed_shard, jnp.where(is_owned, local_ids, 0), axis=0).astype(jnp.bfloat16)
        part_rows = jnp.where(is_owned[:, :, None], owned_rows, jnp.zeros((), jnp.bfloat16))
        x_rows = lax.psum_scatter(part_rows, AXIS_NAME, scatter_dimension=0, tiled=True).astype(jnp.float32)
        gain_full = lax.all_gather(gain_shard, AXIS_NAME, axis=0, tiled=True)
        wq_full = lax.all_gather(wq_shard.astype(jnp.bfloat16), AXIS_NAME, axis=0, tiled=True)
        wk_full = lax.all_gather(wk_shard.astype(jnp.bfloat16), AXIS_NAME, axis=0, tiled=True)
        wv_full = lax.all_gather(wv_shard.astype(jnp.bfloat16), AXIS_NAME, axis=0, tiled=True)
        inv_rms, h_rows, normed = norm_forward(x_rows, gain_full)
        query_proj = jnp.einsum("bsd,df->bsf", normed, wq_full, preferred_element_type=jnp.float32).astype(jnp.bfloat16)
        key_proj = jnp.einsum("bsd,df->bsf", normed, wk_full, preferred_element_type=jnp.float32).astype(jnp.bfloat16)
        value_proj = jnp.einsum("bsd,df->bsf", normed, wv_full, preferred_element_type=jnp.float32).astype(jnp.bfloat16)
        d_w_query = lax.psum_scatter(jnp.einsum("bsd,bsf->df", normed, d_query, preferred_element_type=jnp.float32), AXIS_NAME, scatter_dimension=0, tiled=True)
        d_w_key = lax.psum_scatter(jnp.einsum("bsd,bsf->df", normed, d_key, preferred_element_type=jnp.float32), AXIS_NAME, scatter_dimension=0, tiled=True)
        d_w_value = lax.psum_scatter(jnp.einsum("bsd,bsf->df", normed, d_value, preferred_element_type=jnp.float32), AXIS_NAME, scatter_dimension=0, tiled=True)
        d_normed = (jnp.einsum("bsf,df->bsd", d_query, wq_full, preferred_element_type=jnp.float32)
                    + jnp.einsum("bsf,df->bsd", d_key, wk_full, preferred_element_type=jnp.float32)
                    + jnp.einsum("bsf,df->bsd", d_value, wv_full, preferred_element_type=jnp.float32))
        d_norm_gain = lax.psum_scatter(jnp.sum(d_normed * h_rows, axis=(0, 1)), AXIS_NAME, scatter_dimension=0, tiled=True)
        u_rows = d_normed * gain_full
        d_x = inv_rms * (u_rows - h_rows * jnp.mean(u_rows * h_rows, axis=-1, keepdims=True))
        all_dx = lax.all_gather(d_x, AXIS_NAME, axis=0, tiled=True)
        scatter_ids = jnp.where(is_owned, local_ids, vocab_local)
        d_embed = jnp.zeros(embed_shard.shape, jnp.float32).at[scatter_ids].add(all_dx, mode="drop")
        return (query_proj, key_proj, value_proj, d_embed, d_norm_gain, d_w_query, d_w_key, d_w_value)

    row_spec = P(AXIS_NAME, None)
    act_spec = P(AXIS_NAME, None, None)
    vec_spec = P(AXIS_NAME)
    return jax.shard_map(local_step, mesh=mesh,
                         in_specs=(row_spec, row_spec, vec_spec, row_spec, row_spec, row_spec, act_spec, act_spec, act_spec),
                         out_specs=(act_spec, act_spec, act_spec, row_spec, vec_spec, row_spec, row_spec, row_spec),
                         check_vma=False)
```

profile of v0, /device:TPU:0, one launch (start us, length us, event | category | flops | bytes accessed | tf_op | source)
XLA Modules:
  0.0 785.7 jit_solution(7763954504218213235)
XLA Ops:
  7.2 0.0 copy-start
  7.2 0.0 copy-start.3
  7.2 0.0 all-gather.9.cloned.1.call-start
  7.2 2.9 convert_element_type.42
  10.1 0.0 all-gather.9.cloned.1.call-update
  10.1 0.0 all-gather.7.cloned.1.call-start
  10.2 2.7 convert_element_type.39
  12.9 0.0 all-gather.7.cloned.1.call-update
  12.9 0.0 reduce-scatter.5.cloned.1.call-start
  13.0 0.0 copy-done.3
  13.0 13.8 %all-gather = s32[8,1,512]{2,1,0:T(1,128)S(1)} all-gather(s32[1,1,512]{2,1,0:T(1,128)S(1)} %bitcast.92), channel_id=1, replica_groups=mesh['fsdp'=8] {'fsdp'}, dimensions={0}, use_global_device_ids=true | all-gather | bytes 18432 | tf_op jit(solution)/shard_map/all_gather | solution.py:19
  26.8 46.6 %gather_fusion = bf16[4096,2048]{1,0:T(8,128)(2,1)} fusion(f32[6144,2048]{1,0:T(8,128)} %param.10, s32[4096]{0:T(1024)S(1)} %broadcast_clamp_fusion), kind=kCustom, calls=%fused_computation | custom fusion | bytes 33570816 | tf_op jit(solution)/shard_map/jit(_take)/gather | solution.py:22
  73.5 15.3 %fusion.2 = bf16[8,512,2048]{2,1,0:T(8,128)(2,1)} fusion(bf16[8,512,2048]{2,1,0:T(8,128)(2,1)} %bitcast.78, pred[8,512]{1,0:T(8,128)(4,1)S(1)} %get-tuple-element.13, pred[8,512]{1,0:T(8,128)(4,1)S(1)} %get-tuple-element.12), kind=kLoop, calls=%fused_computation.5 | loop fusion | flops 16777216 | bytes 33562624 | tf_op jit(solution)/shard_map/jit(_where)/select_n | solution.py:23
  88.8 0.0 reduce-scatter.5.cloned.1.call-update
  88.8 0.0 copy-start.4
  88.8 0.0 all-gather.11.cloned.1.call-start
  88.8 2.7 convert_element_type.45
  91.6 0.0 all-gather.11.cloned.1.call-update
  91.6 0.0 all-gather.13.cloned.1.call-start
  91.6 0.0 copy-done.4
  91.6 11.4 %all-gather.1 = f32[8,1,256]{2,1,0:T(1,128)S(1)} all-gather(f32[1,1,256]{2,1,0:T(1,128)S(1)} %bitcast.93), channel_id=1, replica_groups=mesh['fsdp'=8] {'fsdp'}, dimensions={0}, use_global_device_ids=true | all-gather | bytes 9216 | tf_op jit(solution)/shard_map/all_gather | solution.py:25
  103.1 0.0 all-gather.9.cloned.1.call-done
  103.1 10.5 %fusion.22 = f32[512,2048]{1,0:T(8,128)} fusion(bf16[2048,2048]{1,0:T(8,128)(2,1)} %all-gather.9.cloned.1.call-done, bf16[1,512,2048]{2,1,0:T(8,128)(2,1)} %param.16), kind=kOutput, calls=%fused_computation.31 | convolution fusion | flops 4294967296 | bytes 14680064 | tf_op jit(solution)/shard_map/bsf,df->bsd/dot_general | solution.py:37
  113.6 0.0 all-gather.7.cloned.1.call-done
  113.6 10.5 %fusion.26 = f32[512,2048]{1,0:T(8,128)} fusion(bf16[2048,2048]{1,0:T(8,128)(2,1)} %all-gather.7.cloned.1.call-done, bf16[1,512,2048]{2,1,0:T(8,128)(2,1)} %param.15), kind=kOutput, calls=%fused_computation.35 | convolution fusion | flops 4294967296 | bytes 14680064 | tf_op jit(solution)/shard_map/bsf,df->bsd/dot_general | solution.py:36
  124.1 99.6 %reduce-scatter.5.cloned.1.call-done = bf16[1,512,2048]{2,1,0:T(8,128)(2,1)} async-done(((bf16[8,512,2048]{2,1,0:T(8,128)(2,1)}), bf16[1,512,2048]{2,1,0:T(8,128)(2,1)}) %reduce-scatter.5.cloned.1.call-update) | async-done | bytes 2097168 | tf_op jit(solution)/shard_map/reduce_scatter | solution.py:24
  223.7 2.1 fusion.12
  225.8 48.5 %all-gather.11.cloned.1.call-done = bf16[2048,2048]{1,0:T(8,128)(2,1)} async-done(((bf16[256,2048]{1,0:T(8,128)(2,1)}), bf16[2048,2048]{1,0:T(8,128)(2,1)}) %all-gather.11.cloned.1.call-update) | async-done | bytes 8388624 | tf_op jit(solution)/shard_map/all_gather | solution.py:28
  274.4 0.0 copy-done
  274.4 0.0 copy-start.1
  274.4 11.5 %fusion.11 = (f32[2048]{0:T(1024)S(1)}, f32[512]{0:T(512)S(1)}, f32[512,2048]{1,0:T(8,128)S(1)}) fusion(bf16[1,512,2048]{2,1,0:T(8,128)(2,1)} %reduce-scatter.5.cloned.1.call-done, f32[512]{0:T(512)S(1)} %add_rsqrt_fusion, f32[2048]{0:T(1024)S(1)} %bitcast.83, bf16[2048,2048]{1,0:T(8,128)(2,1)} %all-gather.11.cloned.1.call-done, ...), kind=kOutput, calls=%fused_computation.16 | convolution fusion | flops 4304401920 | bytes 25186304 | tf_op jit(solution)/shard_map/bsf,df->bsd/dot_general | solution.py:38
  285.9 0.0 copy-done.1
  285.9 2.9 fusion.10
  288.8 0.0 all-gather.13.cloned.1.call-update
  288.9 0.2 reduce-scatter.7.cloned.1.call-start
  289.1 12.6 %fusion.24 = f32[2048,2048]{1,0:T(8,128)} fusion(bf16[1,512,2048]{2,1,0:T(8,128)(2,1)} %param.15, bf16[1,512,2048]{2,1,0:T(8,128)(2,1)} %reduce-scatter.5.cloned.1.call-done, f32[2048]{0:T(1024)S(1)} %bitcast.85, f32[512]{0:T(512)S(1)} %add_rsqrt_fusion), kind=kOutput, calls=%fused_computation.33 | convolution fusion | flops 4299161600 | bytes 20981760 | tf_op jit(solution)/shard_map/bsd,bsf->df/dot_general | solution.py:33
  301.7 0.0 reduce-scatter.7.cloned.1.call-update
  301.7 0.0 reduce-scatter.9.cloned.1.call-start
  301.8 12.6 %fusion.20 = f32[2048,2048]{1,0:T(8,128)} fusion(bf16[1,512,2048]{2,1,0:T(8,128)(2,1)} %param.16, bf16[1,512,2048]{2,1,0:T(8,128)(2,1)} %reduce-scatter.5.cloned.1.call-done, f32[2048]{0:T(1024)S(1)} %bitcast.86, f32[512]{0:T(512)S(1)} %add_rsqrt_fusion), kind=kOutput, calls=%fused_computation.29 | convolution fusion | flops 4299161600 | bytes 20981760 | tf_op jit(solution)/shard_map/bsd,bsf->df/dot_general | solution.py:34
  314.4 0.0 reduce-scatter.9.cloned.1.call-update
  314.4 0.0 reduce-scatter.11.cloned.1.call-start
  314.5 9.8 %fusion.17 = f32[2048,2048]{1,0:T(8,128)} fusion(bf16[1,512,2048]{2,1,0:T(8,128)(2,1)S(1)} %copy-done, bf16[1,512,2048]{2,1,0:T(8,128)(2,1)} %reduce-scatter.5.cloned.1.call-done, f32[2048]{0:T(1024)S(1)} %bitcast.87, f32[512]{0:T(512)S(1)} %add_rsqrt_fusion), kind=kOutput, calls=%fused_computation.26 | convolution fusion | flops 4299161600 | bytes 20981760 | tf_op jit(solution)/shard_map/bsd,bsf->df/dot_general | solution.py:35
  324.2 0.0 reduce-scatter.11.cloned.1.call-update
  324.3 23.2 %all-reduce = f32[2048]{0:T(1024)S(1)} all-reduce(f32[2048]{0:T(1024)S(1)} %get-tuple-element.8), channel_id=3, replica_groups=mesh['fsdp'=8] {'fsdp'}, use_global_device_ids=true, to_apply=%region_5.6.clone | all-reduce | flops 2048 | bytes 16384
  347.5 0.6 dynamic-slice
  348.1 0.0 copy-start.2
  348.1 0.0 slice-start
  348.1 10.0 %fusion.14 = bf16[1,512,2048]{2,1,0:T(8,128)(2,1)} fusion(bf16[2048,2048]{1,0:T(8,128)(2,1)} %all-gather.9.cloned.1.call-done, bf16[1,512,2048]{2,1,0:T(8,128)(2,1)} %reduce-scatter.5.cloned.1.call-done, f32[2048]{0:T(1024)S(1)} %bitcast.88, f32[512]{0:T(512)S(1)} %add_rsqrt_fusion), kind=kOutput, calls=%fused_computation.23 | convolution fusion | flops 4300210176 | bytes 12593152 | tf_op jit(solution)/shard_map/bsd,df->bsf/dot_general | solution.py:31
  358.1 0.0 copy-done.2
  358.1 0.0 slice-start.1
  358.1 9.4 %fusion.13 = bf16[1,512,2048]{2,1,0:T(8,128)(2,1)} fusion(bf16[2048,2048]{1,0:T(8,128)(2,1)} %all-gather.7.cloned.1.call-done, bf16[1,512,2048]{2,1,0:T(8,128)(2,1)S(1)} %copy-done.2, f32[2048]{0:T(1024)S(1)} %bitcast.89, f32[512]{0:T(512)S(1)} %add_rsqrt_fusion), kind=kOutput, calls=%fused_computation.22 | convolution fusion | flops 4300210176 | bytes 12593152 | tf_op jit(solution)/shard_map/bsd,df->bsf/dot_general | solution.py:30
  367.6 0.0 slice-done
  367.6 0.0 slice-done.1
  367.6 5.8 fusion.15
  373.3 72.3 %all-gather.13.cloned.1.call-done = f32[8,512,2048]{2,1,0:T(8,128)} async-done(((f32[1,512,2048]{2,1,0:T(8,128)}), f32[8,512,2048]{2,1,0:T(8,128)}) %all-gather.13.cloned.1.call-update) | async-done | bytes 33554448 | tf_op jit(solution)/shard_map/all_gather | solution.py:42
  445.7 72.7 %scatter_custom_fusion = f32[6144,2048]{1,0:T(8,128)} fusion(s32[4096]{0:T(1024)S(1)} %bitcast.91, f32[4096,2048]{1,0:T(8,128)} %bitcast.94, f32[]{:T(128)} %constant.15.clone.1), kind=kCustom, calls=%fused_computation.3 | custom fusion | flops 8388608 | bytes 50332160 | tf_op jit(solution)/shard_map/scatter-add | solution.py:44
  518.3 38.2 %reduce-scatter.7.cloned.1.call-done = f32[256,2048]{1,0:T(8,128)} async-done(((f32[2048,2048]{1,0:T(8,128)}), f32[256,2048]{1,0:T(8,128)}) %reduce-scatter.7.cloned.1.call-update) | async-done | bytes 2097168 | tf_op jit(solution)/shard_map/reduce_scatter | solution.py:33
  556.5 111.0 %reduce-scatter.9.cloned.1.call-done = f32[256,2048]{1,0:T(8,128)} async-done(((f32[2048,2048]{1,0:T(8,128)}), f32[256,2048]{1,0:T(8,128)}) %reduce-scatter.9.cloned.1.call-update) | async-done | bytes 2097168 | tf_op jit(solution)/shard_map/reduce_scatter | solution.py:34
  667.6 111.0 %reduce-scatter.11.cloned.1.call-done = f32[256,2048]{1,0:T(8,128)} async-done(((f32[2048,2048]{1,0:T(8,128)}), f32[256,2048]{1,0:T(8,128)}) %reduce-scatter.11.cloned.1.call-update) | async-done | bytes 2097168 | tf_op jit(solution)/shard_map/reduce_scatter | solution.py:35
  (9 shorter events, 0.1 us)
Async XLA Ops:
  7.2 267.2 %copy-start = (bf16[1,512,2048]{2,1,0:T(8,128)(2,1)S(1)}, bf16[1,512,2048]{2,1,0:T(8,128)(2,1)}, u32[]{:S(2)}) copy-start(bf16[1,512,2048]{2,1,0:T(8,128)(2,1)} %param.17) | copy-start | bytes 6291460
  7.2 5.8 copy-start.3
  7.2 95.9 %all-gather.9.cloned.1.call-start = ((), (), s32[]{:S(2)}) async-start(), calls=%async_computation.6 | async-start | bytes 9437184 | tf_op jit(solution)/shard_map/all_gather | solution.py:27
  10.1 103.5 %all-gather.7.cloned.1.call-start = ((), (), s32[]{:S(2)}) async-start(), calls=%async_computation.5 | async-start | bytes 9437184 | tf_op jit(solution)/shard_map/all_gather | solution.py:26
  12.9 210.8 %reduce-scatter.5.cloned.1.call-start = ((), (), s32[]{:S(2)}) async-start(), calls=%async_computation.4 | async-start | bytes 18874368 | tf_op jit(solution)/shard_map/reduce_scatter | solution.py:24
  88.8 2.9 copy-start.4
  88.8 185.6 %all-gather.11.cloned.1.call-start = ((), (), s32[]{:S(2)}) async-start(), calls=%async_computation.7 | async-start | bytes 9437184 | tf_op jit(solution)/shard_map/all_gather | solution.py:28
  91.6 354.1 %all-gather.13.cloned.1.call-start = ((), (), s32[]{:S(2)}) async-start(), calls=%async_computation.8 | async-start | bytes 37748736 | tf_op jit(solution)/shard_map/all_gather | solution.py:42
  274.4 11.6 %copy-start.1 = (bf16[1,512,2048]{2,1,0:T(8,128)(2,1)S(1)}, bf16[1,512,2048]{2,1,0:T(8,128)(2,1)}, u32[]{:S(2)}) copy-start(bf16[1,512,2048]{2,1,0:T(8,128)(2,1)} %reduce-scatter.5.cloned.1.call-done) | copy-start | bytes 6291460
  288.9 267.7 %reduce-scatter.7.cloned.1.call-start = ((), (), s32[]{:S(2)}) async-start(), calls=%async_computation.9 | async-start | bytes 18874368 | tf_op jit(solution)/shard_map/reduce_scatter | solution.py:33
  301.7 365.8 %reduce-scatter.9.cloned.1.call-start = ((), (), s32[]{:S(2)}) async-start(), calls=%async_computation.10 | async-start | bytes 18874368 | tf_op jit(solution)/shard_map/reduce_scatter | solution.py:34
  314.4 464.2 %reduce-scatter.11.cloned.1.call-start = ((), (), s32[]{:S(2)}) async-start(), calls=%async_computation.11 | async-start | bytes 18874368 | tf_op jit(solution)/shard_map/reduce_scatter | solution.py:35
  348.1 10.0 %copy-start.2 = (bf16[1,512,2048]{2,1,0:T(8,128)(2,1)S(1)}, bf16[1,512,2048]{2,1,0:T(8,128)(2,1)}, u32[]{:S(2)}) copy-start(bf16[1,512,2048]{2,1,0:T(8,128)(2,1)} %reduce-scatter.5.cloned.1.call-done) | copy-start | bytes 6291460
  348.1 19.4 %slice-start = ((s8[8388608]{0:T(1024)(128)(4,1)}), s8[4194304]{0:T(1024)(128)(4,1)S(1)}, s32[]{:S(2)}) async-start(s8[8388608]{0:T(1024)(128)(4,1)} %bitcast.95), calls=%async_computation.12 | async-start | bytes 8388608
  358.1 9.4 %slice-start.1 = ((s8[8388608]{0:T(1024)(128)(4,1)}), s8[4194304]{0:T(1024)(128)(4,1)S(1)}, s32[]{:S(2)}) async-start(s8[8388608]{0:T(1024)(128)(4,1)} %bitcast.95), calls=%async_computation.13 | async-start | bytes 8388608
Sparse Core Ops, SparseCore 0:
  10.4 51.3 all-gather.8
  64.1 48.4 all-gather.6
  116.8 106.9 reduce-scatter.4
  226.0 48.3 all-gather.10
  289.0 156.6 all-gather.12
  449.6 106.9 reduce-scatter.6
  560.6 106.9 reduce-scatter.8
  671.6 106.9 reduce-scatter.10
where the time goes:
time: 789 us; the launch traced here: 786 us
  waiting for transfers between devices  481 us (61%)
  other arithmetic  101 us (13%)
  matrix products  92.8 us (12%)
  blocking collectives  48.4 us (6%)
  local copies, waits for them, and re-layouts  47.3 us (6%)
  between operations  14.6 us (2%)
    reduce_scatter x1, waiting for transfers between devices, local_step(): lax.psum_scatter(jnp.einsum('bsd,bsf->df', normed, d_value, preferred_ele...  111 us
    reduce_scatter x1, waiting for transfers between devices, local_step(): lax.psum_scatter(jnp.einsum('bsd,bsf->df', normed, d_key, preferred_eleme...  111 us
    reduce_scatter x1, waiting for transfers between devices, local_step(): lax.psum_scatter(part_rows, AXIS_NAME, scatter_dimension=0, tiled=True)  99.6 us
    scatter-add x1, other arithmetic, local_step(): jnp.zeros(embed_shard.shape, jnp.float32).at[scatter_ids]  72.7 us
    all_gather x1, waiting for transfers between devices, local_step(): all_dx = lax.all_gather(d_x, AXIS_NAME, axis=0, tiled=True)  72.3 us
    all_gather x1, waiting for transfers between devices, local_step(): lax.all_gather(wv_shard.astype(jnp.bfloat16), AXIS_NAME, axis=0, tiled=True)  48.5 us
    gather x1, local copies, waits for them, and re-layouts, local_step(): jnp.take(embed_shard, jnp.where(is_owned, local_ids, 0), axis=0)  46.6 us
    reduce_scatter x1, waiting for transfers between devices, local_step(): lax.psum_scatter(jnp.einsum('bsd,bsf->df', normed, d_query, preferred_ele...  38.2 us
  transfers between devices with their start and end apart: 8, of which 6 were waited for; matrix products, arithmetic and copies ran while one was open for 29% of the time, Pallas kernels for 0%

commit v1 on v0

v1 whole, which is shorter than its diff:
```python
import functools

import jax
import jax.numpy as jnp
from jax import lax
from jax.experimental import pallas as pl
from jax.experimental.pallas import tpu as pltpu
from jax.sharding import PartitionSpec as P

AXIS_NAME = "fsdp"
MAIN_SLOTS = 1920
NUM_CHUNKS = 4
ARRIVALS = ([[(0, c) for c in range(4)], [(1, c) for c in range(4)]]
            + [[(2, k), (4, k), (3, k), (5, k)] for k in range(4)]
            + [[(6, j), (6, j + 2), (7, j), (7, j + 2)] for j in range(2)])


def gather_and_backward_kernel(seq, dim, width3, rows_local, cot_ref, w_ref, n_ref, nst_ref, hs_ref,
                               all_ref, q_ref, dn_ref, dw_ref, dg_ref,
                               w_vm, a_vm, dn_vm, dw_vm, dg_vm,
                               recv_sem, send_sem, w_sem, load_sem, out_sem, q_sem):
    me = lax.axis_index(AXIS_NAME)
    step = seq // NUM_CHUNKS
    width = width3 // 3
    mesh_id = pl.DeviceIdType.MESH

    def remote(src, src_dev, chunk, target, sem):
        return pltpu.make_async_remote_copy(
            src_ref=src, dst_ref=all_ref.at[src_dev, pl.ds(chunk * step, step)],
            send_sem=send_sem.at[sem], recv_sem=recv_sem.at[lax.bitwise_xor(src_dev, target), chunk],
            device_id=(target,), device_id_type=mesh_id)

    def own_copy(mask, chunk):
        return remote(cot_ref.at[pl.ds(chunk * step, step)], me, chunk, me ^ mask, (mask // 2) * NUM_CHUNKS + chunk)

    def forward(mask, chunk, target_mask, sem):
        src_dev = me ^ mask
        return remote(all_ref.at[src_dev, pl.ds(chunk * step, step)], src_dev, chunk, me ^ target_mask, sem)

    def arrived(mask, chunk):
        return pltpu.make_async_remote_copy(
            src_ref=cot_ref.at[pl.ds(0, step)], dst_ref=all_ref.at[me ^ mask, pl.ds(chunk * step, step)],
            send_sem=send_sem.at[0], recv_sem=recv_sem.at[mask, chunk], device_id=(me,), device_id_type=mesh_id)

    barrier = pltpu.get_barrier_semaphore()
    for mask in (1, 2, 4):
        pl.semaphore_signal(barrier, inc=1, device_id=(me ^ mask,), device_id_type=mesh_id)
    pl.semaphore_wait(barrier, 3)

    for chunk in range(NUM_CHUNKS):
        for mask in (2, 4, 1):
            own_copy(mask, chunk).start()

    w_copies = [pltpu.make_async_copy(w_ref, w_vm, w_sem.at[0])]
    for c in w_copies:
        c.start()
    own_load = pltpu.make_async_copy(cot_ref, a_vm.at[0], load_sem.at[0])
    own_load.start()
    dw_vm[...] = jnp.zeros_like(dw_vm)
    dg_vm[...] = jnp.zeros_like(dg_vm)
    for c in w_copies:
        c.wait()

    tile_q = 512

    def q_tile(i, carry):
        cols = pl.ds(pl.multiple_of(i * tile_q, tile_q), tile_q)
        a_vm[1, :, cols] = jnp.dot(n_ref[...], w_vm[:, cols], preferred_element_type=jnp.float32).astype(jnp.bfloat16)
        return carry

    lax.fori_loop(0, width3 // tile_q, q_tile, 0)
    q_copy = [pltpu.make_async_copy(a_vm.at[1, :, pl.ds(i * width, width)], q_ref.at[i], q_sem.at[i]) for i in range(3)]
    for c in q_copy:
        c.start()
    own_load.wait()

    def load_groups(groups, buf):
        copies = [pltpu.make_async_copy(all_ref.at[me ^ mask, pl.ds(chunk * step, step)],
                                        a_vm.at[buf, pl.ds(g * step, step)], load_sem.at[g])
                  for g, (mask, chunk) in enumerate(groups)]
        for c in copies:
            c.start()
        for c in copies:
            c.wait()

    def dn_out(u):
        return pltpu.make_async_copy(dn_vm, dn_ref.at[pl.ds(u * seq, seq)], out_sem.at[0])

    def unit(u, carry):
        buf = u % 2

        @pl.when(u == 1)
        def _():
            for c in q_copy:
                c.wait()
            for chunk in range(NUM_CHUNKS):
                arrived(1, chunk).wait_recv()
            load_groups([(1, c) for c in range(NUM_CHUNKS)], buf)

        @pl.when((u >= 2) & (u < 6))
        def _():
            k = u - 2
            arrived(2, k).wait_recv()
            forward(2, k, 1, 12 + k).start()

            @pl.when(k < 2)
            def _():
                forward(2, k, 4, 24 + k).start()

            arrived(4, k).wait_recv()
            forward(4, k, 1, 16 + k).start()

            @pl.when(k >= 2)
            def _():
                forward(4, k, 2, 24 + k).start()

            arrived(3, k).wait_recv()
            arrived(5, k).wait_recv()
            load_groups([(2, k), (4, k), (3, k), (5, k)], buf)

        @pl.when(u >= 6)
        def _():
            j = u - 6
            for chunk in (j, j + 2):
                arrived(6, chunk).wait_recv()
                forward(6, chunk, 1, 20 + chunk).start()
            for chunk in (j, j + 2):
                arrived(7, chunk).wait_recv()
            load_groups([(6, j), (6, j + 2), (7, j), (7, j + 2)], buf)

        rows = pl.ds(pl.multiple_of(u * seq, seq), seq)
        tile_w = 512

        def dw_tile(i, c):
            cols = pl.ds(pl.multiple_of(i * tile_w, tile_w), tile_w)
            dw_vm[:, cols] += jnp.dot(nst_ref[:, rows], a_vm[buf, :, cols], preferred_element_type=jnp.float32)
            return c

        lax.fori_loop(0, width3 // tile_w, dw_tile, 0)

        @pl.when(u >= 1)
        def _():
            dn_out(u - 1).wait()

        def dn_tile(i, c):
            d_rows = pl.ds(pl.multiple_of(i * rows_local, rows_local), rows_local)
            acc = lax.dot_general(a_vm[buf], w_vm[d_rows, :], (((1,), (1,)), ((), ())), preferred_element_type=jnp.float32)
            dn_vm[:, d_rows] = acc

            @pl.when(i == me)
            def _():
                dg_vm[...] += jnp.sum((acc * hs_ref[rows, :]).reshape(seq // 8, 8, rows_local), axis=0)

            return c

        lax.fori_loop(0, dim // rows_local, dn_tile, 0)
        dn_out(u).start()
        return carry

    lax.fori_loop(0, 8, unit, 0)
    dw_copies = [pltpu.make_async_copy(dw_vm.at[:, pl.ds(i * width, width)], dw_ref.at[i], q_sem.at[i]) for i in range(3)]
    for c in dw_copies:
        c.start()
    dg_ref[...] = dg_vm[...]
    dn_out(7).wait()
    for c in dw_copies:
        c.wait()
    for chunk in range(NUM_CHUNKS):
        for mask in (2, 4, 1):
            own_copy(mask, chunk).wait_send()
        forward(2, chunk, 1, 12 + chunk).wait_send()
        forward(4, chunk, 1, 16 + chunk).wait_send()
        forward(6, chunk, 1, 20 + chunk).wait_send()
        forward(2 if chunk < 2 else 4, chunk, 4 if chunk < 2 else 2, 24 + chunk).wait_send()


def gather_and_backward(cot, w_full, n_home, ns_t, hs_all):
    seq, width3 = cot.shape
    dim = w_full.shape[0]
    rows_local, num_tok = ns_t.shape
    width = width3 // 3
    any_spec = pl.BlockSpec(memory_space=pl.ANY)
    vm_spec = pl.BlockSpec(memory_space=pltpu.VMEM)
    flops = 2 * num_tok * dim * width3 + 2 * num_tok * rows_local * width3 + 2 * seq * dim * width3
    return pl.pallas_call(
        functools.partial(gather_and_backward_kernel, seq, dim, width3, rows_local),
        out_shape=(jax.ShapeDtypeStruct((8, seq, width3), jnp.bfloat16),
                   jax.ShapeDtypeStruct((3, seq, width), jnp.bfloat16),
                   jax.ShapeDtypeStruct((num_tok, dim), jnp.float32),
                   jax.ShapeDtypeStruct((3, rows_local, width), jnp.float32),
                   jax.ShapeDtypeStruct((8, rows_local), jnp.float32)),
        in_specs=[any_spec, any_spec, vm_spec, vm_spec, vm_spec],
        out_specs=(any_spec, any_spec, any_spec, any_spec, vm_spec),
        scratch_shapes=[
            pltpu.VMEM((dim, width3), jnp.bfloat16),
            pltpu.VMEM((2, seq, width3), jnp.bfloat16),
            pltpu.VMEM((seq, dim), jnp.float32),
            pltpu.VMEM((rows_local, width3), jnp.float32),
            pltpu.VMEM((8, rows_local), jnp.float32),
            pltpu.SemaphoreType.DMA((8, NUM_CHUNKS)),
            pltpu.SemaphoreType.DMA((28,)),
            pltpu.SemaphoreType.DMA((1,)),
            pltpu.SemaphoreType.DMA((4,)),
            pltpu.SemaphoreType.DMA((1,)),
            pltpu.SemaphoreType.DMA((3,)),
        ],
        cost_estimate=pl.CostEstimate(flops=flops, bytes_accessed=150_000_000, transcendentals=0),
        compiler_params=pltpu.CompilerParams(collective_id=1, has_side_effects=True, vmem_limit_bytes=67_043_328),
        name="gather_and_backward",
    )(cot, w_full, n_home, ns_t, hs_all)


def solution(mesh):
    num_dev = mesh.shape[AXIS_NAME]

    def local_step(tokens, embed_shard, gain_shard, wq_shard, wk_shard, wv_shard, d_query, d_key, d_value):
        vocab_local, dim = embed_shard.shape
        rows_local, width = wq_shard.shape
        seq = tokens.shape[1]
        num_tok = num_dev * seq
        dev_index = lax.axis_index(AXIS_NAME)

        w_own = jnp.concatenate([wq_shard, wk_shard, wv_shard], axis=1).astype(jnp.bfloat16)
        w_full = lax.all_gather(w_own, AXIS_NAME, axis=0, tiled=True)
        gain_full = lax.all_gather(gain_shard, AXIS_NAME, axis=0, tiled=True)

        ids = lax.all_gather(tokens, AXIS_NAME, axis=0, tiled=True).reshape(num_tok)
        pieces = jnp.asarray([[m, c] for unit in ARRIVALS for m, c in unit], jnp.int32)
        piece_rows = (pieces[:, 0] ^ dev_index) * NUM_CHUNKS + pieces[:, 1]

        def in_arrival_order(per_token):
            return per_token.reshape(num_dev * NUM_CHUNKS, seq // NUM_CHUNKS)[piece_rows].reshape(num_tok)

        pos = jnp.arange(num_tok, dtype=jnp.int32)
        first_pos = jnp.min(jnp.where(ids[:, None] == ids[None, :], pos[None, :], num_tok), axis=1)
        is_first = first_pos == pos
        slot = jnp.sum((is_first[None, :] & (pos[None, :] < first_pos[:, None])).astype(jnp.int32), axis=1)
        num_slots = jnp.sum(is_first.astype(jnp.int32))
        slot_arr = in_arrival_order(slot)
        slot_home = lax.dynamic_slice(slot, (dev_index * seq,), (seq,))

        def rows_of(local_ids):
            owned = (local_ids >= 0) & (local_ids < vocab_local)
            rows = jnp.take(embed_shard, jnp.where(owned, local_ids, 0), axis=0).astype(jnp.bfloat16)
            return owned, jnp.where(owned[:, None], rows, jnp.zeros((), jnp.bfloat16))

        def slot_batch(base, count):
            names = base + jnp.arange(count, dtype=jnp.int32)
            uid = jnp.max(jnp.where(is_first[None, :] & (slot[None, :] == names[:, None]), ids[None, :], -1), axis=1)
            part = rows_of(uid - dev_index * vocab_local)[1]
            x_slots = lax.all_gather(lax.psum_scatter(part, AXIS_NAME, scatter_dimension=0, tiled=True),
                                     AXIS_NAME, axis=0, tiled=True)
            xf = x_slots.astype(jnp.float32)
            inv = lax.rsqrt(jnp.mean(xf * xf, axis=-1, keepdims=True) + 1e-5)
            n_slots = ((xf * inv) * gain_full).astype(jnp.bfloat16)
            hot_home = (slot_home[:, None] == names[None, :]).astype(jnp.bfloat16)
            n_home = jnp.dot(hot_home, n_slots, preferred_element_type=jnp.float32).astype(jnp.bfloat16)
            hot_all = slot_arr[:, None] == names[None, :]
            x_cols = lax.dynamic_slice(x_slots, (0, dev_index * rows_local), (count, rows_local))
            xs_all = jnp.dot(hot_all.astype(jnp.bfloat16), x_cols, preferred_element_type=jnp.float32)
            inv_all = jnp.sum(jnp.where(hot_all, inv[:, 0][None, :], 0.0), axis=1)
            return n_home, xs_all, inv_all

        main = slot_batch(0, MAIN_SLOTS)
        n_home, xs_all, inv_all = lax.cond(
            num_slots > MAIN_SLOTS,
            lambda m: jax.tree.map(jnp.add, m, slot_batch(MAIN_SLOTS, num_tok - MAIN_SLOTS)),
            lambda m: m, main)
        hs_all = xs_all * inv_all[:, None]
        ns_t = (hs_all * gain_shard[None, :]).astype(jnp.bfloat16).T

        cot = jnp.concatenate([d_query[0], d_key[0], d_value[0]], axis=1)
        _, proj, d_normed, d_w, d_gain = gather_and_backward(cot, w_full, n_home, ns_t, hs_all)

        local_ids = in_arrival_order(ids) - dev_index * vocab_local
        owned, x_own = rows_of(local_ids)
        x_own = x_own.astype(jnp.float32)
        inv_own = lax.rsqrt(jnp.mean(x_own * x_own, axis=-1, keepdims=True) + 1e-5)
        h_own = x_own * inv_own
        u_own = d_normed * gain_full
        d_x = inv_own * (u_own - h_own * jnp.mean(u_own * h_own, axis=-1, keepdims=True))
        d_embed = jnp.zeros(embed_shard.shape, jnp.float32).at[jnp.where(owned, local_ids, vocab_local)].add(d_x, mode="drop")
        return (proj[0][None], proj[1][None], proj[2][None], d_embed, jnp.sum(d_gain, axis=0), d_w[0], d_w[1], d_w[2])

    row_spec = P(AXIS_NAME, None)
    act_spec = P(AXIS_NAME, None, None)
    vec_spec = P(AXIS_NAME)
    return jax.shard_map(local_step, mesh=mesh,
                         in_specs=(row_spec, row_spec, vec_spec, row_spec, row_spec, row_spec, act_spec, act_spec, act_spec),
                         out_specs=(act_spec, act_spec, act_spec, row_spec, vec_spec, row_spec, row_spec, row_spec),
                         check_vma=False)
```

time: 789 us -> 742 us (0.940)
  waiting for transfers between devices: 481 us -> 135 us
  Pallas kernels: 0 us -> 240 us
  other arithmetic: 101 us -> 205 us
  matrix products: 92.8 us -> 13.6 us
  local copies, waits for them, and re-layouts: 47.3 us -> 91.6 us
  blocking collectives: 48.4 us -> 24.4 us
  loops' own time: 0 us -> 8.77 us
    reduce_scatter x4 -> x1, waiting for transfers between devices: 360 us -> 60.4 us  [slot_batch(): lax.psum_scatter(part, AXIS_NAME, scatter_dimension=0, tiled=True)]
    pallas_call x0 -> x1, Pallas kernels: none -> 240 us  [gather_and_backward(): pl.pallas_call(functools.partial(gather_and_backward_kernel, seq, dim, wi...]
    dot_general x9 -> x2, matrix products: 92.8 us -> 13.6 us  [the longest x1 8.63 us: slot_batch(): jnp.dot(hot_all.astype(jnp.bfloat16), x_cols, preferred_element_type=jnp....]
    reduce_sum x1 -> x7, other arithmetic: 2.07 us -> 61.1 us  [the longest x1 19.7 us: local_step(): jnp.mean(u_own * h_own, axis=-1, keepdims=True)]
    all_gather x4 -> x2, waiting for transfers between devices: 121 us -> 73.5 us  [the longest x1 43 us: local_step(): w_full = lax.all_gather(w_own, AXIS_NAME, axis=0, tiled=True)]
    gather x1 -> x4, local copies, waits for them, and re-layouts: 46.6 us -> 79.5 us  [the longest x2 78.4 us: rows_of(): jnp.take(embed_shard, jnp.where(owned, local_ids, 0), axis=0)]
    unnamed x1 -> x0, blocking collectives: 23.2 us -> none
    mul x1, other arithmetic: 2.92 us -> 25.3 us  [local_step(): inv_own * (u_own - h_own * jnp.mean(u_own * h_own, axis=-1, keepdims=True))]
  transfers between devices with their start and end apart: 8 -> 3, of which waited for: 6 -> 3; matrix products, arithmetic and copies ran while one was open for 29% -> 11% of each run, Pallas kernels for 0% -> 0%
where the time goes in v1:
time: 742 us; the launch traced here: 733 us
  Pallas kernels  240 us (32%)
  other arithmetic  205 us (28%)
  waiting for transfers between devices  135 us (18%)
  local copies, waits for them, and re-layouts  91.6 us (12%)
  blocking collectives  24.4 us (3%)
  between operations  15.2 us (2%)
  matrix products  13.6 us (2%)
  loops' own time  8.77 us (1%)
    pallas_call x1, Pallas kernels, gather_and_backward(): pl.pallas_call(functools.partial(gather_and_backward_kernel, seq, dim, wi...  240 us
    gather x2, local copies, waits for them, and re-layouts, rows_of(): jnp.take(embed_shard, jnp.where(owned, local_ids, 0), axis=0)  78.4 us
    scatter-add x1, other arithmetic, local_step(): jnp.zeros(embed_shard.shape, jnp.float32)  72.4 us
    reduce_scatter x1, waiting for transfers between devices, slot_batch(): lax.psum_scatter(part, AXIS_NAME, scatter_dimension=0, tiled=True)  60.4 us
    all_gather x1, waiting for transfers between devices, local_step(): w_full = lax.all_gather(w_own, AXIS_NAME, axis=0, tiled=True)  43 us
    all_gather x1, waiting for transfers between devices, slot_batch(): lax.all_gather(lax.psum_scatter(part, AXIS_NAME, scatter_dimension=0, til...  30.4 us
    mul x1, other arithmetic, local_step(): inv_own * (u_own - h_own * jnp.mean(u_own * h_own, axis=-1, keepdims=True))  25.3 us
    reduce_sum x1, other arithmetic, local_step(): jnp.mean(u_own * h_own, axis=-1, keepdims=True)  19.7 us
  transfers between devices with their start and end apart: 3, of which 3 were waited for; matrix products, arithmetic and copies ran while one was open for 11% of the time, Pallas kernels for 0%

profile of v1, /device:TPU:0, one launch (start us, length us, event | category | flops | bytes accessed | tf_op | source)
XLA Modules:
  0.0 732.8 jit_solution(18139387290066526859)
XLA Ops:
  7.2 0.0 reduce-scatter.5.cloned.1.call-start
  7.2 13.6 %all-gather = s32[8,1,512]{2,1,0:T(1,128)S(1)} all-gather(s32[1,1,512]{2,1,0:T(1,128)} %bitcast.65), channel_id=1, replica_groups=mesh['fsdp'=8] {'fsdp'}, dimensions={0}, use_global_device_ids=true | all-gather | bytes 18432 | tf_op jit(solution)/shard_map/all_gather | solution.py:227
  20.8 13.2 %select_reduce_fusion.1 = s32[4096]{0:T(1024)S(1)} fusion(s32[4096]{0:T(1024)S(1)} %bitcast.48), kind=kLoop, calls=%fused_computation.43 | loop fusion | flops 50327552 | bytes 32768 | tf_op jit(solution)/shard_map/reduce_min | solution.py:235
  34.0 0.6 convert_reduce_fusion.1
  34.6 13.3 %convert_reduce_fusion = s32[4096]{0:T(1024)S(1)} fusion(s32[4096]{0:T(1024)S(1)} %select_reduce_fusion.1, pred[4096]{0:T(1024)(128)(4,1)S(1)} %get-tuple-element.73), kind=kLoop, calls=%fused_computation.41 | loop fusion | flops 67104768 | bytes 36864 | tf_op jit(solution)/shard_map/reduce_sum | solution.py:237
  47.9 9.5 %select_reduce_fusion.3 = s32[1920]{0:T(1024)S(1)} fusion(s32[4096]{0:T(1024)S(1)} %bitcast.49, s32[4096]{0:T(1024)S(1)} %convert_reduce_fusion, pred[4096]{0:T(1024)(128)(4,1)S(1)} %get-tuple-element.73), kind=kLoop, calls=%fused_computation.57 | loop fusion | flops 31455360 | bytes 44544 | tf_op jit(solution)/shard_map/reduce_max | solution.py:249
  57.5 31.8 %gather_fusion.1 = bf16[1920,2048]{1,0:T(8,128)(2,1)} fusion(f32[6144,2048]{1,0:T(8,128)} %param.13, s32[2048]{0:T(1024)S(1)} %pad_clamp_fusion.1), kind=kCustom, calls=%fused_computation.1 | custom fusion | bytes 15736320 | tf_op jit(solution)/shard_map/jit(_take)/gather | solution.py:244
  89.2 8.0 %fusion.48 = bf16[1920,2048]{1,0:T(8,128)(2,1)} fusion(bf16[1920,2048]{1,0:T(8,128)(2,1)} %gather_fusion.1, pred[1920]{0:T(1024)(128)(4,1)S(1)} %compare_and_fusion.4, pred[1920]{0:T(1024)(128)(4,1)S(1)} %get-tuple-element.70), kind=kLoop, calls=%fused_computation.70 | loop fusion | flops 7864320 | bytes 15732480 | tf_op jit(solution)/shard_map/jit(_where)/select_n | solution.py:245
  97.2 0.0 reduce-scatter.5.cloned.1.call-update
  97.3 0.0 all-gather.10.cloned.1.call-start
  97.3 60.4 %reduce-scatter.5.cloned.1.call-done = bf16[240,2048]{1,0:T(8,128)(2,1)} async-done(((bf16[1920,2048]{1,0:T(8,128)(2,1)}), bf16[240,2048]{1,0:T(8,128)(2,1)}) %reduce-scatter.5.cloned.1.call-update) | async-done | bytes 983056 | tf_op jit(solution)/shard_map/reduce_scatter | solution.py:251
  157.7 0.0 all-gather.10.cloned.1.call-update
  157.7 0.1 dynamic_slice.9
  158.4 0.0 copy-done.3
  158.4 0.1 convert.10
  158.6 1.7 convert.11
  160.3 1.7 convert.9
  162.1 0.0 copy-done.12
  162.1 0.6 gather_fusion.2
  162.7 0.0 copy-done.11
  162.7 10.9 %all-gather.1 = f32[8,1,256]{2,1,0:T(1,128)S(1)} all-gather(f32[1,1,256]{2,1,0:T(1,128)S(1)} %bitcast.64), channel_id=1, replica_groups=mesh['fsdp'=8] {'fsdp'}, dimensions={0}, use_global_device_ids=true | all-gather | bytes 9216 | tf_op jit(solution)/shard_map/all_gather | solution.py:225
  173.6 1.8 pad_maximum_fusion.1
  175.4 30.4 %all-gather.10.cloned.1.call-done = bf16[1920,2048]{1,0:T(8,128)(2,1)} async-done(((bf16[240,2048]{1,0:T(8,128)(2,1)}), bf16[1920,2048]{1,0:T(8,128)(2,1)}) %all-gather.10.cloned.1.call-update) | async-done | bytes 7864336 | tf_op jit(solution)/shard_map/all_gather | solution.py:251
  205.8 5.0 fusion.44
  210.8 4.1 select_reduce_fusion.2
  215.0 8.6 %fusion.39 = f32[4096,256]{1,0:T(8,128)} fusion(s32[4096]{0:T(1024)S(1)} %bitcast.60, bf16[1920,2048]{1,0:T(8,128)(2,1)} %all-gather.10.cloned.1.call-done, s32[]{:T(128)S(6)} %select_n.181), kind=kOutput, calls=%fused_computation.56 | convolution fusion | flops 4034396160 | bytes 5193732 | tf_op jit(solution)/shard_map/dot_general | solution.py:260
  223.6 4.9 fusion.53
  228.6 0.0 copy-done.8
  228.6 8.8 %conditional.1 = ((bf16[512,2048]{1,0:T(8,128)(2,1)S(1)}, f32[4096,256]{1,0:T(8,128)}, f32[4096]{0:T(1024)S(1)})) conditional(s32[]{:T(128)} %convert_element_type.48, (bf16[512,2048]{1,0:T(8,128)(2,1)S(1)}, f32[4096,256]{1,0:T(8,128)}, f32[4096]{0:T(1024)S(1)}) %tuple.15, (s32[512]{0:T(512)S(1)}, pred[4096]{0:T(1024)(128)(4,1)S(1)}, ...), branch_computations={%region_7.8_spmd, %region_8.13_spmd} | conditional | flops 9242527744 | bytes 163314912 | solution.py:265
  237.4 0.0 copy-start.14
  237.4 0.0 all-gather.8.cloned.1.call-start
  237.4 0.7 all-gather.8.cloned.1.call-update
  238.1 0.6 copy-done.14
  238.7 0.6 gather_fusion.3
  239.3 0.6 compare_select_fusion.3
  239.9 46.6 %gather_fusion.4 = bf16[4096,2048]{1,0:T(8,128)(2,1)} fusion(f32[6144,2048]{1,0:T(8,128)} %param.13, s32[4096]{0:T(1024)S(1)} %broadcast_clamp_fusion), kind=kCustom, calls=%fused_computation.4 | custom fusion | bytes 33570816 | tf_op jit(solution)/shard_map/jit(_take)/gather | solution.py:244
  286.6 0.0 copy-start.4
  286.6 0.0 copy-start.5
  286.6 0.0 copy-start.6
  286.6 17.8 %fusion.38 = (f32[4096]{0:T(1024)S(1)}, bf16[4096,2048]{1,0:T(8,128)(2,1)}) fusion(bf16[4096,2048]{1,0:T(8,128)(2,1)} %gather_fusion.4, pred[4096]{0:T(1024)(128)(4,1)S(1)} %compare_and_fusion.3, pred[4096]{0:T(1024)(128)(4,1)S(1)} %get-tuple-element.66), kind=kLoop, calls=%fused_computation.52 | loop fusion | flops 41938944 | bytes 33579008 | tf_op jit(solution)/shard_map/reduce_sum | solution.py:278
  304.4 0.6 add_rsqrt_fusion.1
  305.0 0.0 copy-done.4
  305.1 0.0 copy-done.6
  305.1 6.4 pad_maximum_fusion.cot_ref
  311.4 2.4 fusion.56
  313.8 2.8 copy.21.nst_ref
  316.7 43.0 %all-gather.8.cloned.1.call-done.w_ref = bf16[2048,6144]{1,0:T(8,128)(2,1)} async-done(((bf16[256,6144]{1,0:T(8,128)(2,1)}), bf16[2048,6144]{1,0:T(8,128)(2,1)}) %all-gather.8.cloned.1.call-update) | async-done | bytes 25165840 | tf_op jit(solution)/shard_map/all_gather | solution.py:224
  359.7 239.5 %gather_and_backward.1 = (bf16[8,512,6144]{2,1,0:T(8,128)(2,1)}, bf16[3,512,2048]{2,1,0:T(8,128)(2,1)}, f32[4096,2048]{1,0:T(8,128)}, f32[3,256,2048]{2,1,0:T(8,128)}, f32[8,256]{1,0:T(8,128)}) custom-call(bf16[512,6144]{1,0:T(8,128)(2,1)} %pad_maximum_fusion.cot_ref, bf16[2048,6144]{1,0:T(8,128)(2,1)} %all-gather.8.cloned.1.call-done.w_ref, ...), custom_call_target="tpu_custom_call" | custom-call | flops 128849018880 | bytes 150000000 | tf_op jit(solution)/shard_map/gather_and_backward/pallas_call | solution.py:185
  599.2 0.0 copy-start
  599.3 0.0 copy-start.7
  599.3 0.0 copy-start.9
  599.3 0.0 slice-start.4
  599.3 19.7 %fusion.35 = f32[4096]{0:T(1024)S(1)} fusion(bf16[4096,2048]{1,0:T(8,128)(2,1)} %get-tuple-element.65, f32[4096,2048]{1,0:T(8,128)} %get-tuple-element.58, f32[2048]{0:T(1024)} %bitcast.56, f32[4096]{0:T(1024)} %add_rsqrt_fusion.1), kind=kLoop, calls=%fused_computation.49 | loop fusion | flops 41938944 | bytes 50372608 | tf_op jit(solution)/shard_map/reduce_sum | solution.py:281
  619.0 0.4 copy-done
  619.5 0.0 copy-done.9
  619.5 25.3 %fusion.37 = f32[4096,2048]{1,0:T(8,128)} fusion(bf16[4096,2048]{1,0:T(8,128)(2,1)S(1)} %copy-done, f32[4096,2048]{1,0:T(8,128)} %get-tuple-element.58, f32[4096]{0:T(1024)S(1)} %broadcast_multiply_fusion.1, f32[2048]{0:T(1024)S(1)} %bitcast.57, f32[4096]{0:T(1024)S(1)} %copy-done.7), kind=kLoop, calls=%fused_computation.51 | loop fusion | flops 50331648 | bytes 83927040 | tf_op jit(solution)/shard_map/mul | solution.py:281
  644.8 0.0 slice-start.2
  644.8 0.0 slice-start.3
  644.8 3.4 slice_bitcast_fusion
  648.2 1.0 slice-done.2
  649.2 0.7 slice-done.3
  649.8 2.9 fusion.66
  652.8 0.6 reduce_sum.87
  653.4 72.4 %scatter_custom_fusion = f32[6144,2048]{1,0:T(8,128)} fusion(s32[4096]{0:T(1024)} %bitcast.63, f32[4096,2048]{1,0:T(8,128)} %fusion.37, f32[]{:T(128)} %constant.30.clone.1), kind=kCustom, calls=%fused_computation.60 | custom fusion | flops 8388608 | bytes 50332160 | tf_op jit(solution)/shard_map/scatter-add | solution.py:282
  (33 shorter events, 0.2 us)
Async XLA Ops:
  7.2 150.5 %reduce-scatter.5.cloned.1.call-start = ((), (), s32[]{:S(2)}) async-start(), calls=%async_computation.5 | async-start | bytes 8847360 | tf_op jit(solution)/shard_map/reduce_scatter | solution.py:251
  89.2 69.2 %copy-start.3 = (f32[256,2048]{1,0:T(8,128)S(1)}, f32[256,2048]{1,0:T(8,128)}, u32[]{:S(2)}) copy-start(f32[256,2048]{1,0:T(8,128)} %param.16) | copy-start | bytes 6291460
  97.2 64.9 %copy-start.12 = (s32[32,1]{0,1:T(1,128)S(1)}, s32[32,1]{0,1:T(1,128)}, u32[]{:S(2)}) copy-start(s32[32,1]{0,1:T(1,128)} %constant.119) | copy-start | bytes 388
  97.2 64.9 %copy-start.13 = (s32[32,1]{0,1:T(1,128)S(1)}, s32[32,1]{0,1:T(1,128)}, u32[]{:S(2)}) copy-start(s32[32,1]{0,1:T(1,128)} %constant.120) | copy-start | bytes 388
  97.2 65.5 %copy-start.11 = (f32[256]{0:T(256)S(1)}, f32[256]{0:T(256)}, u32[]{:S(2)}) copy-start(f32[256]{0:T(256)} %param.14) | copy-start | bytes 3076
  97.3 108.6 %all-gather.10.cloned.1.call-start = ((), (), s32[]{:S(2)}) async-start(), calls=%async_computation.6 | async-start | bytes 8847360 | tf_op jit(solution)/shard_map/all_gather | solution.py:251
  173.6 55.0 %copy-start.8 = (f32[8,1,256]{2,1,0:T(1,128)}, f32[8,1,256]{2,1,0:T(1,128)S(1)}, u32[]{:S(2)}) copy-start(f32[8,1,256]{2,1,0:T(1,128)S(1)} %all-gather.1) | copy-start | bytes 24580
  205.8 17.8 %slice-start = ((s8[7864320]{0:T(1024)(128)(4,1)}), s8[3670016]{0:T(1024)(128)(4,1)S(1)}, s32[]{:S(2)}) async-start(s8[7864320]{0:T(1024)(128)(4,1)} %bitcast.39), calls=%async_computation.7 | async-start | bytes 7340032
  215.0 8.7 %slice-start.1 = ((s8[7864320]{0:T(1024)(128)(4,1)}), s8[4194304]{0:T(1024)(128)(4,1)S(1)}, s32[]{:S(2)}) async-start(s8[7864320]{0:T(1024)(128)(4,1)} %bitcast.39), calls=%async_computation.8 | async-start | bytes 8388608
  237.4 1.3 copy-start.14
  237.4 122.3 %all-gather.8.cloned.1.call-start = ((), (), s32[]{:S(2)}) async-start(), calls=%async_computation.4 | async-start | bytes 28311552 | tf_op jit(solution)/shard_map/all_gather | solution.py:224
  286.6 18.4 %copy-start.4 = (bf16[1,512,2048]{2,1,0:T(8,128)(2,1)S(1)}, bf16[1,512,2048]{2,1,0:T(8,128)(2,1)}, u32[]{:S(2)}) copy-start(bf16[1,512,2048]{2,1,0:T(8,128)(2,1)} %param.20) | copy-start | bytes 6291460
  286.6 18.4 %copy-start.5 = (bf16[1,512,2048]{2,1,0:T(8,128)(2,1)S(1)}, bf16[1,512,2048]{2,1,0:T(8,128)(2,1)}, u32[]{:S(2)}) copy-start(bf16[1,512,2048]{2,1,0:T(8,128)(2,1)} %param.19) | copy-start | bytes 6291460
  286.6 18.4 %copy-start.6 = (bf16[1,512,2048]{2,1,0:T(8,128)(2,1)S(1)}, bf16[1,512,2048]{2,1,0:T(8,128)(2,1)}, u32[]{:S(2)}) copy-start(bf16[1,512,2048]{2,1,0:T(8,128)(2,1)} %param.18) | copy-start | bytes 6291460
  304.4 7.0 copy-start.2
  599.2 20.2 %copy-start = (bf16[4096,2048]{1,0:T(8,128)(2,1)S(1)}, bf16[4096,2048]{1,0:T(8,128)(2,1)}, u32[]{:S(2)}) copy-start(bf16[4096,2048]{1,0:T(8,128)(2,1)} %get-tuple-element.65) | copy-start | bytes 50331652
  599.3 20.2 %copy-start.7 = (f32[4096]{0:T(1024)S(1)}, f32[4096]{0:T(1024)}, u32[]{:S(2)}) copy-start(f32[4096]{0:T(1024)} %add_rsqrt_fusion.1) | copy-start | bytes 49156
  599.3 20.2 %copy-start.9 = (f32[8,1,256]{2,1,0:T(1,128)S(1)}, f32[8,1,256]{2,1,0:T(1,128)}, u32[]{:S(2)}) copy-start(f32[8,1,256]{2,1,0:T(1,128)} %copy-done.8) | copy-start | bytes 24580
  599.3 45.5 %slice-start.4 = ((s8[6291456]{0:T(1024)(128)(4,1)}), s8[4194304]{0:T(1024)(128)(4,1)S(1)}, s32[]{:S(2)}) async-start(s8[6291456]{0:T(1024)(128)(4,1)} %bitcast.43), calls=%async_computation.11 | async-start | bytes 8388608
  619.5 25.3 %slice-start.5 = ((s8[6291456]{0:T(1024)(128)(4,1)}), s8[2097152]{0:T(1024)(128)(4,1)S(1)}, s32[]{:S(2)}) async-start(s8[6291456]{0:T(1024)(128)(4,1)} %bitcast.43), calls=%async_computation.12 | async-start | bytes 4194304
  644.8 4.4 slice-start.2
  644.8 5.1 slice-start.3
  648.2 4.6 copy-start.10
Sparse Core Ops, SparseCore 0:
  97.4 60.2 reduce-scatter.4
  159.5 46.2 all-gather.9
  240.0 119.6 all-gather.7
